TPU v7x, 512 devices: a whole 4x4x16 slice. The times are simulated.
512 devices in a mesh: grp: 4 (over x), dom: 128 (over z, y, core).
Axes of the slice: x: 4, y: 4, z: 16, core: 2. Of those that a mesh axis runs over, the one named last changes fastest.
Arguments:
- node_state: float32 [65536, 6, 128], P(('grp', 'dom')), may hold values from -6 to 6
- node_dest: int32 [65536], P(('grp', 'dom')), may hold values from 0 to 127, as said below
- seg_nodes: float32 [6, 262144], P(None, ('grp', 'dom')), may hold values from -6 to 6
- seg_conn: int32 [3, 524288], P(None, ('grp', 'dom')), may hold values from 0 to 511
- pair_seg: int32 [512, 4, 32], P(('grp', 'dom')), may hold values from 0 to 7
- pair_slot: int32 [512, 4, 32], P(('grp', 'dom')), may hold values from 0 to 255, as said below
Outputs:
- node_force: float32 [65536, 3, 128], P(('grp', 'dom'))
Inputs may be any that keep to these rules, and one draw needn't show every extreme that they name: `node_dest`: at most 2 blocks of one device name the same contact domain; in every grp row one contact domain receives exactly 2 blocks from every device of that row; every device sends at least one block to the contact domain of its own dom index. `pair_slot`: every entry names a slot d * 2 + k that holds a block: device (r, d) sends more than k blocks to the contact domain.
All inputs are finite; a program needn't handle non-finite values.
Results may differ from a plain program's by a relative error of at most 0.00023.
Values sent between devices are 32-bit elements; how exact they have to be, the bound alone decides.
No kernel may reach another device: no remote copies, remote signals or barrier semaphores. Data moves between devices by JAX's collectives and lax.ppermute only.
A program may use at most 64 MiB of HBM per device.

v0:
```python
import jax
import jax.numpy as jnp
from jax import lax
from jax.sharding import Mesh
from jax.sharding import PartitionSpec as P

SEG_BLK = 128
DOM = ("dom_0", "dom_1", "dom_2")
GRP_DOM = ("grp", "dom_0", "dom_1", "dom_2")
time_step = 0.5
stiffness = 0.5
radius_sq = 0.5


def in_blocks(shard, dim, devices):
    dims = shard.shape
    blocks = shard.reshape(*dims[:dim], devices, dims[dim] // devices, *dims[dim + 1 :])
    return jnp.moveaxis(blocks, dim, 0)


def in_order(blocks, dim):
    blocks = jnp.moveaxis(blocks, 0, dim)
    dims = blocks.shape
    return blocks.reshape(*dims[:dim], dims[dim] * dims[dim + 1], *dims[dim + 2 :])


def moved_by_axis(blocks, axes, turns):
    dims = [lax.axis_size(a) for a in axes]
    blocks = blocks.reshape(*dims, *blocks.shape[1:])
    for k in turns:
        blocks = lax.all_to_all(blocks, axes[k], split_axis=k, concat_axis=k, tiled=True)
    return blocks.reshape(-1, *blocks.shape[len(axes) :])


def two_step_exchange(shard, groups, turns, split_dim, concat_dim):
    devices = lax.axis_size(groups[0]) * lax.axis_size(groups[1])
    blocks = in_blocks(shard, split_dim, devices)
    return in_order(moved_by_axis(blocks, groups, turns), concat_dim)


def seg_geometry(corners):
    corner_a = corners[:, 0]
    corner_b = corners[:, 1]
    corner_c = corners[:, 2]
    edge_one = corner_b[0:3] - corner_a[0:3]
    edge_two = corner_c[0:3] - corner_a[0:3]
    normal = 0.5 * jnp.stack(
        [
            edge_one[1] * edge_two[2] - edge_one[2] * edge_two[1],
            edge_one[2] * edge_two[0] - edge_one[0] * edge_two[2],
            edge_one[0] * edge_two[1] - edge_one[1] * edge_two[0],
        ]
    )
    centre = (corner_a[0:3] + corner_b[0:3] + corner_c[0:3]) / 3.0
    motion = (corner_a[3:6] + corner_b[3:6] + corner_c[3:6]) / 3.0
    return jnp.concatenate([normal, centre, motion], axis=0)


def tile_force(node_rows, geometry):
    clearance = jnp.zeros((geometry.shape[1], node_rows.shape[1]), jnp.float32)
    distance = jnp.zeros((geometry.shape[1], node_rows.shape[1]), jnp.float32)
    for axis_id in range(3):
        offset = node_rows[axis_id][None, :] - geometry[3 + axis_id][:, None]
        drift = node_rows[3 + axis_id][None, :] - geometry[6 + axis_id][:, None]
        clearance = clearance + geometry[axis_id][:, None] * (offset + time_step * drift)
        distance = distance + offset * offset
    pressure = stiffness * jnp.exp(-distance / radius_sq) * jnp.maximum(-clearance, 0.0)
    return jnp.dot(
        geometry[0:3], pressure, precision=lax.Precision.HIGHEST, preferred_element_type=jnp.float32
    )


def place_rows(slot_ids, values, slot_total):
    onehot = (slot_ids[None, :] == jnp.arange(slot_total, dtype=jnp.int32)[:, None]).astype(
        jnp.float32
    )
    flattened = values.reshape(values.shape[0], -1)
    placed = jnp.dot(
        onehot, flattened, precision=lax.Precision.HIGHEST, preferred_element_type=jnp.float32
    )
    return placed.reshape((slot_total,) + values.shape[1:])


def shards(node_state, node_dest, seg_nodes, seg_conn, pair_seg, pair_slot):
    dom_count = lax.axis_size(DOM)
    grp_count = lax.axis_size("grp")
    block_count = node_state.shape[0]
    capacity = max(2, 2 * block_count // dom_count)
    slot_count = dom_count * capacity
    order_ids = jnp.arange(block_count, dtype=jnp.int32)
    earlier = order_ids[None, :] < order_ids[:, None]
    same_dom = node_dest[:, None] == node_dest[None, :]
    slot_rank = jnp.sum((same_dom & earlier).astype(jnp.int32), axis=1)
    target_slot = node_dest * capacity + slot_rank
    outgoing = place_rows(target_slot, node_state, slot_count)
    received = two_step_exchange(outgoing, (("dom_0", "dom_1"), "dom_2"), (1, 0), 0, 0)
    corners = jnp.take(seg_nodes, seg_conn, axis=1)
    geometry = seg_geometry(corners)
    seg_blocks = geometry.shape[1] // SEG_BLK
    geo_blocks = jnp.transpose(geometry.reshape(9, seg_blocks, SEG_BLK), (1, 0, 2))
    seg_table = pair_seg[0]
    slot_table = pair_slot[0]
    geo_all = lax.all_gather(geo_blocks, "grp", axis=0, tiled=True)
    seg_in, slot_in = (
        lax.all_to_all(seg_table, "grp", split_axis=0, concat_axis=0, tiled=True),
        lax.all_to_all(slot_table, "grp", split_axis=0, concat_axis=0, tiled=True),
    )
    owner_base = (jnp.arange(grp_count, dtype=jnp.int32) * seg_blocks)[:, None]
    seg_ids = (seg_in + owner_base).reshape(-1)
    slot_ids = slot_in.reshape(-1)
    forces = jax.vmap(tile_force)(
        jnp.take(received, slot_ids, axis=0), jnp.take(geo_all, seg_ids, axis=0)
    )
    own_forces = place_rows(slot_ids, forces, slot_count)
    returned = lax.all_to_all(own_forces, DOM, split_axis=0, concat_axis=0, tiled=True)
    return jnp.take(returned, target_slot, axis=0)


def solution(mesh):
    split = Mesh(
        mesh.devices.reshape(mesh.shape["grp"], 16, 4, 2), ("grp", "dom_0", "dom_1", "dom_2")
    )
    placed = (
        P(GRP_DOM, None, None),
        P(GRP_DOM),
        P(None, GRP_DOM),
        P(None, GRP_DOM),
        P(GRP_DOM, None, None),
        P(GRP_DOM, None, None),
    )
    return jax.shard_map(
        shards, mesh=split, in_specs=placed, out_specs=P(GRP_DOM, None, None), check_vma=False
    )
```

profile of v0, /device:TPU:33, one launch (start us, length us, event | category | flops | bytes accessed | tf_op | source)
XLA Modules:
  0.0 168.8 jit_solution(1052670801400604042)
XLA Ops:
  0.0 0.9 convert_reduce_fusion
  0.9 0.7 compare_and_fusion.3
  1.6 1.2 copy.65
  2.7 0.0 copy-start
  2.8 0.5 fusion.34
  3.3 4.7 %all_to_all.39 = f32[64,2,2,6,128]{4,0,3,2,1:T(8,128)S(1)} all-to-all(f32[64,2,2,6,128]{4,0,3,2,1:T(8,128)S(1)} %fusion.34), channel_id=1, replica_groups=mesh['grp'=4,'dom_0'=16,'dom_1'=4,'dom_2'=2] {'dom_2'}, dimensions={1} | all-to-all | bytes 1572864 | tf_op jit(solution)/shard_map/all_to_all | solution.py:31
  8.0 4.0 %all-to-all-start.1 = ((s32[4,1,32]{2,1,0:T(1,128)}), s32[4,1,32]{2,1,0:T(1,128)S(1)}, u32[]{:S(2)}, u32[]{:S(2)}) async-start(s32[4,1,32]{2,1,0:T(1,128)} %bitcast.4), calls=%async_computation.1 | async-start | bytes 4096 | tf_op jit(solution)/shard_map/all_to_all | solution.py:105
  12.0 0.0 copy-done
  12.0 4.0 %all-to-all-done.1 = s32[4,1,32]{2,1,0:T(1,128)S(1)} async-done(((s32[4,1,32]{2,1,0:T(1,128)}), s32[4,1,32]{2,1,0:T(1,128)S(1)}, u32[]{:S(2)}, u32[]{:S(2)}) %all-to-all-start.1) | async-done | bytes 544 | tf_op jit(solution)/shard_map/all_to_all | solution.py:105
  16.0 3.2 %all-to-all-start = ((s32[4,1,32]{2,1,0:T(1,128)}), s32[4,1,32]{2,1,0:T(1,128)S(1)}, u32[]{:S(2)}, u32[]{:S(2)}) async-start(s32[4,1,32]{2,1,0:T(1,128)} %bitcast.1), calls=%async_computation | async-start | bytes 4096 | tf_op jit(solution)/shard_map/all_to_all | solution.py:106
  19.3 0.0 copy-start.1
  19.3 1.5 copy.66
  20.8 2.5 %all-to-all-done = s32[4,1,32]{2,1,0:T(1,128)S(1)} async-done(((s32[4,1,32]{2,1,0:T(1,128)}), s32[4,1,32]{2,1,0:T(1,128)S(1)}, u32[]{:S(2)}, u32[]{:S(2)}) %all-to-all-start) | async-done | bytes 544 | tf_op jit(solution)/shard_map/all_to_all | solution.py:106
  23.3 17.8 %all-to-all-start.3 = ((f32[64,2,2,6,128]{4,2,3,1,0:T(2,128)}), f32[64,2,2,6,128]{4,2,3,1,0:T(2,128)S(1)}, u32[]{:S(2)}, u32[]{:S(2)}) async-start(f32[64,2,2,6,128]{4,2,3,1,0:T(2,128)} %copy.66), calls=%async_computation.3 | async-start | bytes 1572864 | tf_op jit(solution)/shard_map/all_to_all | solution.py:31
  41.1 0.1 add.137
  41.2 0.1 add.148
  41.3 0.1 add.138
  41.4 0.0 copy-done.1
  41.4 0.1 copy.62
  41.5 8.1 %gather_fusion = f32[3072,6]{1,0:T(8,128)S(1)} fusion(f32[6,512]{0,1:T(8,128)S(1)} %copy.62, s32[3072]{0:T(1024)S(1)} %broadcast_clamp_fusion), kind=kCustom, calls=%fused_computation | custom fusion | bytes 159744 | tf_op jit(solution)/shard_map/jit(_take)/gather | solution.py:97
  49.6 0.5 copy.63
  50.3 9.9 %all_gather.3 = f32[32,9,128]{2,0,1:T(8,128)S(1)} all-gather(f32[8,9,128]{2,0,1:T(8,128)S(1)} %maximum_bitcast_fusion), channel_id=1, replica_groups=mesh['grp'=4,'dom_0'=16,'dom_1'=4,'dom_2'=2] {'grp'}, dimensions={0}, use_global_device_ids=true | all-gather | bytes 184320 | tf_op jit(solution)/shard_map/all_gather | solution.py:103
  60.1 0.1 copy.64
  60.2 0.1 all_to_all.30
  60.3 0.5 broadcast.150
  60.8 0.7 reduce.10
  61.5 0.1 all_to_all.29
  61.6 0.1 reshape.189
  61.7 0.7 reduce.11
  62.3 0.1 eq.61
  62.4 0.8 gather_fusion.1
  63.3 0.2 broadcast_select_fusion
  63.5 0.4 fusion.54
  63.9 16.5 %all-to-all-done.3 = f32[64,2,2,6,128]{4,2,3,1,0:T(2,128)S(1)} async-done(((f32[64,2,2,6,128]{4,2,3,1,0:T(2,128)}), f32[64,2,2,6,128]{4,2,3,1,0:T(2,128)S(1)}, u32[]{:S(2)}, u32[]{:S(2)}) %all-to-all-start.3) | async-done | bytes 786464 | tf_op jit(solution)/shard_map/all_to_all | solution.py:31
  80.4 0.3 copy.67
  80.7 0.5 copy.68
  81.1 0.8 gather_fusion.2
  81.9 0.2 broadcast_select_fusion.1
  82.1 0.3 fusion.55
  82.4 37.2 %fusion.14 = f32[128,3,128]{2,1,0:T(4,128)S(1)} fusion(f32[128,128]{1,0:T(8,128)S(1)} %bitcast.77, f32[128,128]{1,0:T(8,128)S(1)} %bitcast.86, f32[128,128]{1,0:T(8,128)S(1)} %bitcast.78, f32[128,128]{1,0:T(8,128)S(1)} %bitcast.79, f32[128,128]{1,0:T(8,128)S(1)} %bitcast.87, f32[128,128]{1,0:T(8,128)S(1)} %bitcast.80, f32[128,128]{1,0:T(8,128)S(1)} %bitcast.81, ...), kind=kOutput, calls=%fused_computation.24 | convolution fusion | flops 134217728 | bytes 1441792 | tf_op jit(solution)/shard_map/vmap()/dot_general | solution.py:68
  119.6 0.1 copy.69
  119.8 0.3 fusion.37
  120.1 1.1 copy.70
  121.2 12.2 %all-to-all-start.4 = ((f32[256,3,128]{2,1,0:T(4,128)}), f32[256,3,128]{2,1,0:T(4,128)S(1)}, u32[]{:S(2)}, u32[]{:S(2)}) async-start(f32[256,3,128]{2,1,0:T(4,128)} %copy.70), calls=%async_computation.4 | async-start | bytes 1048576 | tf_op jit(solution)/shard_map/all_to_all | solution.py:115
  133.5 33.7 %all-to-all-done.4 = f32[256,3,128]{2,1,0:T(4,128)S(1)} async-done(((f32[256,3,128]{2,1,0:T(4,128)}), f32[256,3,128]{2,1,0:T(4,128)S(1)}, u32[]{:S(2)}, u32[]{:S(2)}) %all-to-all-start.4) | async-done | bytes 393248 | tf_op jit(solution)/shard_map/all_to_all | solution.py:115
  167.1 0.8 gather_fusion.3
  167.9 0.2 broadcast_select_fusion.2
  168.1 0.7 copy.71
  (20 shorter events, 0.2 us)
Async XLA Ops:
  2.7 9.2 %copy-start = (s32[3,1024]{1,0:T(4,128)S(1)}, s32[3,1024]{1,0:T(4,128)}, u32[]{:S(2)}) copy-start(s32[3,1024]{1,0:T(4,128)} %param.9) | copy-start | bytes 36868
  8.0 8.1 %all-to-all-start.1 = ((s32[4,1,32]{2,1,0:T(1,128)}), s32[4,1,32]{2,1,0:T(1,128)S(1)}, u32[]{:S(2)}, u32[]{:S(2)}) async-start(s32[4,1,32]{2,1,0:T(1,128)} %bitcast.4), calls=%async_computation.1 | async-start | bytes 4096 | tf_op jit(solution)/shard_map/all_to_all | solution.py:105
  16.0 7.3 %all-to-all-start = ((s32[4,1,32]{2,1,0:T(1,128)}), s32[4,1,32]{2,1,0:T(1,128)S(1)}, u32[]{:S(2)}, u32[]{:S(2)}) async-start(s32[4,1,32]{2,1,0:T(1,128)} %bitcast.1), calls=%async_computation | async-start | bytes 4096 | tf_op jit(solution)/shard_map/all_to_all | solution.py:106
  19.3 22.1 %copy-start.1 = (f32[6,512]{1,0:T(8,128)S(1)}, f32[6,512]{1,0:T(8,128)}, u32[]{:S(2)}) copy-start(f32[6,512]{1,0:T(8,128)} %param.8) | copy-start | bytes 36868
  23.3 57.1 %all-to-all-start.3 = ((f32[64,2,2,6,128]{4,2,3,1,0:T(2,128)}), f32[64,2,2,6,128]{4,2,3,1,0:T(2,128)S(1)}, u32[]{:S(2)}, u32[]{:S(2)}) async-start(f32[64,2,2,6,128]{4,2,3,1,0:T(2,128)} %copy.66), calls=%async_computation.3 | async-start | bytes 1572864 | tf_op jit(solution)/shard_map/all_to_all | solution.py:31
  121.2 46.0 %all-to-all-start.4 = ((f32[256,3,128]{2,1,0:T(4,128)}), f32[256,3,128]{2,1,0:T(4,128)S(1)}, u32[]{:S(2)}, u32[]{:S(2)}) async-start(f32[256,3,128]{2,1,0:T(4,128)} %copy.70), calls=%async_computation.4 | async-start | bytes 1048576 | tf_op jit(solution)/shard_map/all_to_all | solution.py:115
where the time goes:
time: 169 us
  waiting for transfers between devices  56.7 us (34%)
  matrix products  38.1 us (23%)
  starting transfers between devices  37.3 us (22%)
  local copies, waits for them, and re-layouts  18.2 us (11%)
  blocking collectives  14.5 us (9%)
  other arithmetic  3.67 us (2%)
    dot_general x1, matrix products, tile_force(): jnp.dot(geometry[0:3], pressure, precision=lax.Precision.HIGHEST, preferr...  37.2 us
    all_to_all x1, waiting for transfers between devices, shards(): lax.all_to_all(own_forces, DOM, split_axis=0, concat_axis=0, tiled=True)  33.7 us
    all_to_all x1, starting transfers between devices, moved_by_axis(): lax.all_to_all(blocks, axes[k], split_axis=k, concat_axis=k, tiled=True)  17.8 us
    all_to_all x1, waiting for transfers between devices, moved_by_axis(): lax.all_to_all(blocks, axes[k], split_axis=k, concat_axis=k, tiled=True)  16.5 us
    all_to_all x1, starting transfers between devices, shards(): lax.all_to_all(own_forces, DOM, split_axis=0, concat_axis=0, tiled=True)  12.2 us
    all_gather x1, blocking collectives, shards(): geo_all = lax.all_gather(geo_blocks, 'grp', axis=0, tiled=True)  9.87 us
    gather x2, local copies, waits for them, and re-layouts, shards(): corners = jnp.take(seg_nodes, seg_conn, axis=1)  8.59 us
    all_to_all x1, blocking collectives, moved_by_axis(): lax.all_to_all(blocks, axes[k], split_axis=k, concat_axis=k, tiled=True)  4.67 us
  transfers between devices with their start and end apart: 4, of which 4 were waited for; matrix products, arithmetic and copies ran while one was open for 8% of the time, Pallas kernels for 0%

commit v1 on v0

--- a/solution.py
+++ b/solution.py
@@ -10,6 +10,28 @@
 time_step = 0.5
 stiffness = 0.5
 radius_sq = 0.5
+
+
+def in_blocks_2(array, dim, size):
+    before, after = (array.shape[:dim], array.shape[dim + 1 :])
+    return jnp.moveaxis(array.reshape(*before, size, -1, *after), dim, 0)
+
+
+def in_order_2(parts, dim):
+    parts = jnp.moveaxis(parts, 0, dim)
+    lengths = parts.shape
+    return parts.reshape(*lengths[:dim], lengths[dim] * lengths[dim + 1], *lengths[dim + 2 :])
+
+
+def sent_to_each(x, axis, split_dim, concat_dim):
+    devices, place = (lax.axis_size(axis), lax.axis_index(axis))
+    blocks = in_blocks_2(x, split_dim, devices)
+    done = [blocks[place]]
+    for step in range(1, devices):
+        sent = blocks[(place + step) % devices]
+        done.append(lax.ppermute(sent, axis, [(i, (i + step) % devices) for i in range(devices)]))
+    blocks = jnp.stack(done)[(place - jnp.arange(devices)) % devices]
+    return in_order_2(blocks, concat_dim)
 
 
 def in_blocks(shard, dim, devices):
@@ -102,7 +124,7 @@
     slot_table = pair_slot[0]
     geo_all = lax.all_gather(geo_blocks, "grp", axis=0, tiled=True)
     seg_in, slot_in = (
-        lax.all_to_all(seg_table, "grp", split_axis=0, concat_axis=0, tiled=True),
+        sent_to_each(seg_table, "grp", 0, 0),
         lax.all_to_all(slot_table, "grp", split_axis=0, concat_axis=0, tiled=True),
     )
     owner_base = (jnp.arange(grp_count, dtype=jnp.int32) * seg_blocks)[:, None]

time: 169 us -> 175 us (1.036)
  starting transfers between devices: 37.3 us -> 41.5 us
  waiting for transfers between devices: 56.7 us -> 54.3 us
    ppermute x0 -> x3, starting transfers between devices: none -> 10.1 us  [sent_to_each(): lax.ppermute(sent, axis, [(i, (i + step) % devices) for i in range(device...]
    all_to_all x1, waiting for transfers between devices: 16.5 us -> 20.6 us  [moved_by_axis(): lax.all_to_all(blocks, axes[k], split_axis=k, concat_axis=k, tiled=True)]
    all_to_all x1 -> x0, waiting for transfers between devices: 4.03 us -> none  [shards(): lax.all_to_all(seg_table, 'grp', split_axis=0, concat_axis=0, tiled=True)]
    all_to_all x1 -> x0, starting transfers between devices: 4.01 us -> none  [shards(): lax.all_to_all(seg_table, 'grp', split_axis=0, concat_axis=0, tiled=True)]
    all_to_all x1, starting transfers between devices: 12.2 us -> 9.48 us  [shards(): lax.all_to_all(own_forces, DOM, split_axis=0, concat_axis=0, tiled=True)]
    all_to_all x1, waiting for transfers between devices: 2.51 us -> 0.01 us  [shards(): lax.all_to_all(slot_table, 'grp', split_axis=0, concat_axis=0, tiled=True)]
  transfers between devices with their start and end apart: 4 -> 6, of which waited for: 4 -> 2; matrix products, arithmetic and copies ran while one was open for 8% -> 11% of each run, Pallas kernels for 0% -> 0%
where the time goes in v1:
time: 175 us; the launch traced here: 174 us
  waiting for transfers between devices  54.3 us (31%)
  starting transfers between devices  41.5 us (24%)
  matrix products  38.1 us (22%)
  local copies, waits for them, and re-layouts  19.3 us (11%)
  blocking collectives  16.1 us (9%)
  other arithmetic  4.53 us (3%)
    dot_general x1, matrix products, tile_force(): jnp.dot(geometry[0:3], pressure, precision=lax.Precision.HIGHEST, preferr...  37.2 us
    all_to_all x1, waiting for transfers between devices, shards(): lax.all_to_all(own_forces, DOM, split_axis=0, concat_axis=0, tiled=True)  33.7 us
    all_to_all x1, waiting for transfers between devices, moved_by_axis(): lax.all_to_all(blocks, axes[k], split_axis=k, concat_axis=k, tiled=True)  20.6 us
    all_to_all x1, starting transfers between devices, moved_by_axis(): lax.all_to_all(blocks, axes[k], split_axis=k, concat_axis=k, tiled=True)  17.8 us
    ppermute x3, starting transfers between devices, sent_to_each(): lax.ppermute(sent, axis, [(i, (i + step) % devices) for i in range(device...  10.1 us
    all_gather x1, blocking collectives, shards(): geo_all = lax.all_gather(geo_blocks, 'grp', axis=0, tiled=True)  10 us
    all_to_all x1, starting transfers between devices, shards(): lax.all_to_all(own_forces, DOM, split_axis=0, concat_axis=0, tiled=True)  9.48 us
    gather x2, local copies, waits for them, and re-layouts, shards(): corners = jnp.take(seg_nodes, seg_conn, axis=1)  8.6 us
  transfers between devices with their start and end apart: 6, of which 2 were waited for; matrix products, arithmetic and copies ran while one was open for 11% of the time, Pallas kernels for 0%

profile of v1, /device:TPU:33, one launch (start us, length us, event | category | flops | bytes accessed | tf_op | source)
XLA Modules:
  0.0 174.2 jit_solution(1197932957835070772)
XLA Ops:
  0.0 4.0 %all-to-all-start = ((s32[4,1,32]{2,1,0:T(1,128)}), s32[4,1,32]{2,1,0:T(1,128)S(1)}, u32[]{:S(2)}, u32[]{:S(2)}) async-start(s32[4,1,32]{2,1,0:T(1,128)} %bitcast.104), calls=%async_computation | async-start | bytes 4096 | tf_op jit(solution)/shard_map/all_to_all | solution.py:128
  4.0 0.8 constant_dynamic-slice_fusion.3
  4.8 3.4 %collective-permute-start = (s32[1,32]{1,0:T(1,128)S(1)}, s32[1,32]{1,0:T(1,128)S(1)}, u32[]{:S(2)}, u32[]{:S(2)}) collective-permute-start(s32[1,32]{1,0:T(1,128)S(1)} %get-tuple-element.30), channel_id=1, source_target_pairs={{0,128},{128,256},{256,384},{384,0},{1,129},{129,257},{257,385},{3... | collective-permute-start | bytes 392 | tf_op jit(solution)/shard_map/ppermute | solution.py:32
  8.2 3.1 %collective-permute-start.2 = (s32[1,32]{1,0:T(1,128)S(1)}, s32[1,32]{1,0:T(1,128)S(1)}, u32[]{:S(2)}, u32[]{:S(2)}) collective-permute-start(s32[1,32]{1,0:T(1,128)S(1)} %get-tuple-element.31), channel_id=1, source_target_pairs={{0,384},{128,0},{256,128},{384,256},{1,385},{129,1},{257,129},{385... | collective-permute-start | bytes 392 | tf_op jit(solution)/shard_map/ppermute | solution.py:32
  11.4 3.7 %collective-permute-start.1 = (s32[1,32]{1,0:T(1,128)S(1)}, s32[1,32]{1,0:T(1,128)S(1)}, u32[]{:S(2)}, u32[]{:S(2)}) collective-permute-start(s32[1,32]{1,0:T(1,128)S(1)} %get-tuple-element.32), channel_id=1, source_target_pairs={{0,256},{128,384},{256,0},{384,128},{1,257},{129,385},{257,1},{385... | collective-permute-start | bytes 392 | tf_op jit(solution)/shard_map/ppermute | solution.py:32
  15.0 0.7 compare_and_fusion
  15.8 0.7 compare_select_fusion
  16.5 0.9 convert_reduce_fusion
  17.4 1.2 copy.62
  18.6 0.0 all-to-all-done
  18.6 0.5 broadcast.217
  19.1 0.7 reduce.5
  19.8 0.1 eq.67
  19.9 0.7 compare_and_fusion.3
  20.6 0.5 fusion.34
  21.1 6.1 %all_to_all.24 = f32[64,2,2,6,128]{4,0,3,2,1:T(8,128)S(1)} all-to-all(f32[64,2,2,6,128]{4,0,3,2,1:T(8,128)S(1)} %fusion.34), channel_id=1, replica_groups=mesh['grp'=4,'dom_0'=16,'dom_1'=4,'dom_2'=2] {'dom_2'}, dimensions={1} | all-to-all | bytes 1572864 | tf_op jit(solution)/shard_map/all_to_all | solution.py:53
  27.1 1.5 copy.63
  28.6 17.8 %all-to-all-start.2 = ((f32[64,2,2,6,128]{4,2,3,1,0:T(2,128)}), f32[64,2,2,6,128]{4,2,3,1,0:T(2,128)S(1)}, u32[]{:S(2)}, u32[]{:S(2)}) async-start(f32[64,2,2,6,128]{4,2,3,1,0:T(2,128)} %copy.63), calls=%async_computation.2 | async-start | bytes 1572864 | tf_op jit(solution)/shard_map/all_to_all | solution.py:53
  46.5 0.1 copy.59
  46.6 8.1 %gather_fusion.1 = f32[3072,6]{1,0:T(8,128)S(1)} fusion(f32[6,512]{0,1:T(8,128)S(1)} %copy.59, s32[3072]{0:T(1024)S(1)} %broadcast_clamp_fusion), kind=kCustom, calls=%fused_computation.1 | custom fusion | bytes 159744 | tf_op jit(solution)/shard_map/jit(_take)/gather | solution.py:119
  54.8 0.5 copy.60
  55.4 10.0 %all_gather.3 = f32[32,9,128]{2,0,1:T(8,128)S(1)} all-gather(f32[8,9,128]{2,0,1:T(8,128)S(1)} %maximum_bitcast_fusion), channel_id=1, replica_groups=mesh['grp'=4,'dom_0'=16,'dom_1'=4,'dom_2'=2] {'grp'}, dimensions={0}, use_global_device_ids=true | all-gather | bytes 184320 | tf_op jit(solution)/shard_map/all_gather | solution.py:125
  65.4 0.1 copy.61
  65.5 0.0 collective-permute-done.2
  65.5 0.0 collective-permute-done.1
  65.6 0.6 gather_fusion
  66.1 0.1 broadcast_add_fusion
  66.2 0.1 reshape.299
  66.3 0.1 reshape.298
  66.4 0.8 gather_fusion.2
  67.2 0.2 broadcast_select_fusion
  67.4 0.4 fusion.59
  67.8 0.1 reshape.249
  67.9 20.6 %all-to-all-done.2 = f32[64,2,2,6,128]{4,2,3,1,0:T(2,128)S(1)} async-done(((f32[64,2,2,6,128]{4,2,3,1,0:T(2,128)}), f32[64,2,2,6,128]{4,2,3,1,0:T(2,128)S(1)}, u32[]{:S(2)}, u32[]{:S(2)}) %all-to-all-start.2) | async-done | bytes 786464 | tf_op jit(solution)/shard_map/all_to_all | solution.py:53
  88.5 0.3 copy.64
  88.8 0.5 copy.65
  89.3 0.8 gather_fusion.3
  90.0 0.2 broadcast_select_fusion.1
  90.2 0.3 fusion.60
  90.5 37.2 %fusion.14 = f32[128,3,128]{2,1,0:T(4,128)S(1)} fusion(f32[128,128]{1,0:T(8,128)S(1)} %bitcast.86, f32[128,128]{1,0:T(8,128)S(1)} %bitcast.95, f32[128,128]{1,0:T(8,128)S(1)} %bitcast.87, f32[128,128]{1,0:T(8,128)S(1)} %bitcast.88, f32[128,128]{1,0:T(8,128)S(1)} %bitcast.96, f32[128,128]{1,0:T(8,128)S(1)} %bitcast.89, f32[128,128]{1,0:T(8,128)S(1)} %bitcast.90, ...), kind=kOutput, calls=%fused_computation.25 | convolution fusion | flops 134217728 | bytes 1441792 | tf_op jit(solution)/shard_map/vmap()/dot_general | solution.py:90
  127.7 0.1 copy.66
  127.9 0.3 fusion.37
  128.2 1.1 copy.67
  129.3 9.5 %all-to-all-start.3 = ((f32[256,3,128]{2,1,0:T(4,128)}), f32[256,3,128]{2,1,0:T(4,128)S(1)}, u32[]{:S(2)}, u32[]{:S(2)}) async-start(f32[256,3,128]{2,1,0:T(4,128)} %copy.67), calls=%async_computation.3 | async-start | bytes 1048576 | tf_op jit(solution)/shard_map/all_to_all | solution.py:137
  138.8 33.7 %all-to-all-done.3 = f32[256,3,128]{2,1,0:T(4,128)S(1)} async-done(((f32[256,3,128]{2,1,0:T(4,128)}), f32[256,3,128]{2,1,0:T(4,128)S(1)}, u32[]{:S(2)}, u32[]{:S(2)}) %all-to-all-start.3) | async-done | bytes 393248 | tf_op jit(solution)/shard_map/all_to_all | solution.py:137
  172.5 0.8 gather_fusion.4
  173.2 0.2 broadcast_select_fusion.2
  173.5 0.7 copy.68
  (23 shorter events, 0.2 us)
Async XLA Ops:
  0.0 18.6 %all-to-all-start = ((s32[4,1,32]{2,1,0:T(1,128)}), s32[4,1,32]{2,1,0:T(1,128)S(1)}, u32[]{:S(2)}, u32[]{:S(2)}) async-start(s32[4,1,32]{2,1,0:T(1,128)} %bitcast.104), calls=%async_computation | async-start | bytes 4096 | tf_op jit(solution)/shard_map/all_to_all | solution.py:128
  4.8 60.7 %collective-permute-start = (s32[1,32]{1,0:T(1,128)S(1)}, s32[1,32]{1,0:T(1,128)S(1)}, u32[]{:S(2)}, u32[]{:S(2)}) collective-permute-start(s32[1,32]{1,0:T(1,128)S(1)} %get-tuple-element.30), channel_id=1, source_target_pairs={{0,128},{128,256},{256,384},{384,0},{1,129},{129,257},{257,385},{3... | collective-permute-start | bytes 392 | tf_op jit(solution)/shard_map/ppermute | solution.py:32
  8.2 57.3 %collective-permute-start.2 = (s32[1,32]{1,0:T(1,128)S(1)}, s32[1,32]{1,0:T(1,128)S(1)}, u32[]{:S(2)}, u32[]{:S(2)}) collective-permute-start(s32[1,32]{1,0:T(1,128)S(1)} %get-tuple-element.31), channel_id=1, source_target_pairs={{0,384},{128,0},{256,128},{384,256},{1,385},{129,1},{257,129},{385... | collective-permute-start | bytes 392 | tf_op jit(solution)/shard_map/ppermute | solution.py:32
  11.4 54.2 %collective-permute-start.1 = (s32[1,32]{1,0:T(1,128)S(1)}, s32[1,32]{1,0:T(1,128)S(1)}, u32[]{:S(2)}, u32[]{:S(2)}) collective-permute-start(s32[1,32]{1,0:T(1,128)S(1)} %get-tuple-element.32), channel_id=1, source_target_pairs={{0,256},{128,384},{256,0},{384,128},{1,257},{129,385},{257,1},{385... | collective-permute-start | bytes 392 | tf_op jit(solution)/shard_map/ppermute | solution.py:32
  27.1 19.4 %copy-start = (f32[6,512]{1,0:T(8,128)S(1)}, f32[6,512]{1,0:T(8,128)}, u32[]{:S(2)}) copy-start(f32[6,512]{1,0:T(8,128)} %param.8) | copy-start | bytes 36868
  28.6 59.9 %all-to-all-start.2 = ((f32[64,2,2,6,128]{4,2,3,1,0:T(2,128)}), f32[64,2,2,6,128]{4,2,3,1,0:T(2,128)S(1)}, u32[]{:S(2)}, u32[]{:S(2)}) async-start(f32[64,2,2,6,128]{4,2,3,1,0:T(2,128)} %copy.63), calls=%async_computation.2 | async-start | bytes 1572864 | tf_op jit(solution)/shard_map/all_to_all | solution.py:53
  129.3 43.2 %all-to-all-start.3 = ((f32[256,3,128]{2,1,0:T(4,128)}), f32[256,3,128]{2,1,0:T(4,128)S(1)}, u32[]{:S(2)}, u32[]{:S(2)}) async-start(f32[256,3,128]{2,1,0:T(4,128)} %copy.67), calls=%async_computation.3 | async-start | bytes 1048576 | tf_op jit(solution)/shard_map/all_to_all | solution.py:137
